TPU v7x, 32 devices: a whole 2x2x4 slice. The times are simulated.
32 devices in a mesh: expert: 2 (over x), dp: 16 (over z, y, core).
Axes of the slice: x: 2, y: 2, z: 4, core: 2. Of those that a mesh axis runs over, the one named last changes fastest.
Arguments:
- features: bfloat16 [4096, 512], P(('expert', 'dp')), may hold values from -31 to 31
- gradients: bfloat16 [4096, 512], P(('expert', 'dp')), may hold values from -31 to 31
- route_ids: int32 [4096, 2], P(('expert', 'dp')), may hold values from 0 to 7, all different within a row; in each aligned block of 128 rows (0 to 127, 128 to 255, ...) at most 64 rows name the same one
- gate_share: float32 [4096], P(('expert', 'dp')), may hold values from 0.5 to 0.95
- token_mask: int32 [4096], P(('expert', 'dp')), may hold values 0 or 1
- damping: float32 [8, 2, 1], P('expert'), may hold values from 0.5 to 2
Outputs:
- act_inverse: float32 [8, 1, 512, 512], P(None, None, 'dp')
- grad_inverse: float32 [8, 1, 512, 512], P(None, None, 'dp')
Inputs may be any that keep to these rules, and one draw needn't show every extreme that they name: `route_ids`: each token names two different experts. Among the 128 tokens of one device no expert is named by more than 64 tokens, a bound that some block reaches.
All inputs are finite; a program needn't handle non-finite values. Where the computation divides by a largest or mean magnitude, that divisor is 1e-20 or more. No bound on the sum of `token_mask` on one device may be relied on, other than what follows from the above.
Results may differ from a plain program's by a relative error of at most 0.0003.
Values may be sent and summed in bfloat16 or wider, within the bound.
No kernel may reach another device: no remote copies, remote signals or barrier semaphores. Data moves between devices by JAX's collectives and lax.ppermute only.
A program may use at most 64 MiB of HBM per device.

v0:
```python
import jax
import jax.numpy as jnp
from jax import lax
from jax.sharding import PartitionSpec as P

EXPERTS = 8
TOP = 2
BLOCK = 512
NBLK = 1
CAP = 64
WIDTH = 512


def slot_table(route_ids, capacity):
    pair_experts = route_ids.reshape(-1)
    onehot = (pair_experts[:, None] == jnp.arange(EXPERTS, dtype=jnp.int32)[None, :]).astype(
        jnp.int32
    )
    running = jnp.cumsum(onehot, axis=0)
    position = jnp.sum(onehot * running, axis=1) - 1
    target = pair_experts * capacity + position
    sources = jnp.arange(1, pair_experts.shape[0] + 1, dtype=jnp.int32)
    return jnp.zeros((EXPERTS * capacity,), jnp.int32).at[target].set(sources)


def newton_rows(rows_now, matrix, whole_now):
    left_product = jnp.einsum("eirk,eikc->eirc", rows_now, matrix, precision=lax.Precision.HIGHEST)
    return 2.0 * rows_now - jnp.einsum(
        "eirk,eikc->eirc", left_product, whole_now, precision=lax.Precision.HIGHEST
    )


def first_iterate(matrix, identity, inverse_bound):
    bound_scale = inverse_bound[:, :, None, None]
    return 2.0 * bound_scale * identity - bound_scale * bound_scale * matrix


def on_device(features, gradients, route_ids, gate_share, token_mask, damping):
    tokens_here = features.shape[0]
    capacity = CAP
    blocks = 2 * NBLK
    kept_mask = token_mask.astype(jnp.float32)
    weight_pair = jnp.stack([gate_share, 1.0 - gate_share], axis=1) * kept_mask[:, None]
    kept_rows = features * token_mask.astype(jnp.bfloat16)[:, None]
    pair_grads = (gradients[:, None, :].astype(jnp.float32) * weight_pair[:, :, None]).astype(
        jnp.bfloat16
    )
    repeated = jnp.broadcast_to(kept_rows[:, None, :], pair_grads.shape)
    pair_rows = jnp.concatenate([repeated, pair_grads], axis=2).reshape(
        tokens_here * TOP, 2 * WIDTH
    )
    padded = jnp.concatenate([jnp.zeros((1, 2 * WIDTH), jnp.bfloat16), pair_rows], axis=0)
    buffer = jnp.take(padded, slot_table(route_ids, capacity), axis=0).reshape(
        EXPERTS, capacity, blocks, BLOCK
    )
    load_inverse = 1.0 / (
        tokens_here * lax.axis_size("expert") * lax.axis_size("dp") * TOP / EXPERTS
    )
    received = lax.all_to_all(buffer, "expert", split_axis=0, concat_axis=1, tiled=True)
    gram_blocks = (
        jnp.einsum("erib,eric->eibc", received, received, preferred_element_type=jnp.float32)
        * load_inverse
    )
    damping_flat = damping.reshape(damping.shape[0], blocks)[:, :, None, None]
    rows_share = BLOCK // lax.axis_size("dp")
    row_start = lax.axis_index("dp") * rows_share
    identity = jnp.eye(BLOCK, dtype=jnp.float32)
    summed = lax.psum(gram_blocks, "dp")
    matrix = summed + damping_flat * identity
    largest_sum = jnp.max(jnp.sum(jnp.abs(matrix), axis=3), axis=2)
    inverse_bound = 1.0 / largest_sum
    iterate_one = first_iterate(matrix, identity, inverse_bound)
    iterate_two = newton_rows(iterate_one, matrix, iterate_one)
    second_rows = lax.dynamic_slice_in_dim(iterate_two, row_start, rows_share, 2)
    third_rows = newton_rows(second_rows, matrix, iterate_two)
    act_rows = third_rows[:, :NBLK]
    grad_rows = third_rows[:, NBLK:]
    act_inverse, grad_inverse = (
        lax.all_gather(act_rows, "expert", axis=0, tiled=True),
        lax.all_gather(grad_rows, "expert", axis=0, tiled=True),
    )
    return (act_inverse, grad_inverse)


def solution(mesh):
    placed = (
        P(("expert", "dp"), None),
        P(("expert", "dp"), None),
        P(("expert", "dp"), None),
        P(("expert", "dp")),
        P(("expert", "dp")),
        P("expert", None, None),
    )
    return jax.shard_map(
        on_device,
        mesh=mesh,
        in_specs=placed,
        out_specs=(P(None, None, "dp", None), P(None, None, "dp", None)),
        check_vma=False,
    )
```

profile of v0, /device:TPU:0, one launch (start us, length us, event | category | flops | bytes accessed | tf_op | source)
XLA Modules:
  0.0 298.0 jit_solution(7920612828320791945)
XLA Ops:
  7.2 0.0 all-reduce.3.cloned.1.call-start
  7.2 0.8 copy.37
  8.0 0.1 eq.38
  8.1 0.1 eq.34
  8.3 0.7 broadcast_multiply_fusion.3
  9.0 0.6 reduce-window.6
  9.6 0.2 slice_reduce_fusion
  9.8 0.1 fusion.18
  9.9 0.1 copy.36
  10.0 0.1 mul.132
  10.2 1.4 scatter_custom_fusion
  11.6 0.7 fusion.25
  12.4 0.1 mul.138
  12.4 0.1 mul.139
  12.6 0.7 subtract_bitcast_fusion
  13.2 0.7 pad_maximum_fusion
  13.9 0.1 copy.39
  14.0 0.1 stack.14
  14.2 1.0 mul.136
  15.2 0.4 mul.137
  15.6 1.0 broadcast_multiply_fusion.1
  16.6 0.1 broadcast_in_dim.36
  16.7 0.1 concatenate.12
  16.8 0.1 multiply_convert_fusion
  17.0 0.1 fusion.16
  17.1 2.1 gather_fusion
  19.2 0.8 gather.7
  20.0 0.1 broadcast_in_dim.19
  20.0 0.2 copy_select_fusion
  20.2 17.7 %all_to_all.18 = bf16[8,64,2,512]{3,1,2,0:T(8,128)(2,1)S(1)} all-to-all(bf16[8,64,2,512]{3,1,2,0:T(8,128)(2,1)S(1)} %copy_select_fusion), channel_id=1, replica_groups=mesh['expert'=2,'dp'=16] {'expert'}, dimensions={0} | all-to-all | bytes 2097152 | tf_op jit(solution)/shard_map/all_to_all | solution.py:59
  38.0 0.1 copy.41
  38.1 4.5 %broadcast_multiply_fusion = f32[4,2,512,512]{3,2,1,0:T(8,128)} fusion(bf16[4,128,2,512]{3,1,2,0:T(8,128)(2,1)S(1)} %bitcast.23), kind=kOutput, calls=%fused_computation.19 | convolution fusion | flops 538968064 | bytes 9437184 | tf_op jit(solution)/shard_map/erib,eric->eibc/dot_general | solution.py:61
  42.6 0.1 copy.43
  42.7 0.1 fusion.15
  42.8 170.4 %all-reduce.3.cloned.1.call-done = f32[4,2,512,512]{3,2,1,0:T(8,128)} async-done(((f32[4,2,512,512]{3,2,1,0:T(8,128)}), f32[4,2,512,512]{3,2,1,0:T(8,128)}) %all-reduce.3.cloned.1.call-update) | async-done | bytes 8388624 | tf_op jit(solution)/shard_map/psum | solution.py:68
  213.2 4.6 %abs_reduce_fusion = f32[4,2,512]{2,1,0:T(2,128)S(1)} fusion(f32[4,2,512,512]{3,2,1,0:T(8,128)} %all-reduce.3.cloned.1.call-done, f32[512,512]{1,0:T(8,128)S(1)} %fusion.15, f32[4,2]{1,0:T(4,128)S(1)} %copy.43), kind=kLoop, calls=%fused_computation.6 | loop fusion | flops 8384512 | bytes 9453600 | tf_op jit(solution)/shard_map/reduce_sum | solution.py:70
  217.8 0.1 reduce_max.9
  217.9 0.1 copy.48
  218.0 0.1 copy.45
  218.1 0.1 copy.46
  218.2 23.3 %fusion.1 = f32[4,2,512,512]{3,2,1,0:T(8,128)} fusion(f32[4,2,512,512]{3,2,1,0:T(8,128)} %all-reduce.3.cloned.1.call-done, f32[4,2]{1,0:T(4,128)S(1)} %copy.46, f32[4,2]{1,0:T(4,128)S(1)} %copy.45, f32[512,512]{1,0:T(8,128)S(1)} %fusion.15, f32[4,2]{1,0:T(4,128)S(1)} %copy.43), kind=kOutput, calls=%fused_computation.5 | convolution fusion | flops 12899581952 | bytes 17825888 | tf_op jit(solution)/shard_map/eirk,eikc->eirc/dot_general | solution.py:27
  241.5 19.9 %multiply_subtract_fusion = f32[4,2,512,512]{3,2,1,0:T(8,128)} fusion(f32[4,2,512,512]{3,2,1,0:T(8,128)} %fusion.1, f32[4,2,512,512]{3,2,1,0:T(8,128)S(1)} %copy-done, f32[4,2]{1,0:T(4,128)S(1)} %copy.46, f32[4,2]{1,0:T(4,128)S(1)} %copy.45, f32[512,512]{1,0:T(8,128)S(1)} %fusion.15, f32[4,2]{1,0:T(4,128)S(1)} %copy.43), kind=kOutput, calls=%fused_computation.2 | convolution fusion | flops 12910067712 | bytes 26214496 | tf_op jit(solution)/shard_map/eirk,eikc->eirc/dot_general | solution.py:28
  261.4 6.8 %fusion.2 = f32[4,2,32,512]{3,2,1,0:T(8,128)S(1)} fusion(f32[4,2,512,512]{3,2,1,0:T(8,128)S(1)} %copy-done, f32[512,512]{1,0:T(8,128)S(1)} %fusion.15, f32[4,2]{1,0:T(4,128)S(1)} %copy.43, f32[4,2,512,512]{3,2,1,0:T(8,128)} %multiply_subtract_fusion, s32[]{:T(128)S(6)} %select_n.26), kind=kOutput, calls=%fused_computation.8 | convolution fusion | flops 809500672 | bytes 10485796 | tf_op jit(solution)/shard_map/eirk,eikc->eirc/dot_general | solution.py:27
  268.2 4.9 %convolution_subtract_fusion = f32[4,2,32,512]{3,2,1,0:T(8,128)S(1)} fusion(f32[4,2,32,512]{3,2,1,0:T(8,128)S(1)} %fusion.2, f32[4,2,512,512]{3,2,1,0:T(8,128)S(1)} %copy-done.1, s32[]{:T(128)S(6)} %select_n.26), kind=kOutput, calls=%fused_computation.20 | convolution fusion | flops 805568512 | bytes 9961476 | tf_op jit(solution)/shard_map/eirk,eikc->eirc/dot_general | solution.py:28
  273.1 8.7 %all_gather.6 = f32[8,1,32,512]{3,2,1,0:T(8,128)S(1)} all-gather(f32[4,1,32,512]{3,2,1,0:T(8,128)S(1)} %get-tuple-element.3), channel_id=1, replica_groups=mesh['expert'=2,'dp'=16] {'expert'}, dimensions={0}, use_global_device_ids=true | all-gather | bytes 786432 | tf_op jit(solution)/shard_map/all_gather | solution.py:79
  281.8 7.8 %all_gather.7 = f32[8,1,32,512]{3,2,1,0:T(8,128)S(1)} all-gather(f32[4,1,32,512]{3,2,1,0:T(8,128)S(1)} %get-tuple-element.2), channel_id=1, replica_groups=mesh['expert'=2,'dp'=16] {'expert'}, dimensions={0}, use_global_device_ids=true | all-gather | bytes 786432 | tf_op jit(solution)/shard_map/all_gather | solution.py:80
  289.6 0.8 copy.53
  290.4 0.8 copy.54
  (19 shorter events, 0.2 us)
Async XLA Ops:
  7.2 206.0 %all-reduce.3.cloned.1.call-start = ((), (), s32[]{:S(2)}) async-start(), calls=%async_computation.1 | async-start | bytes 16777216 | tf_op jit(solution)/shard_map/psum | solution.py:68
  38.1 4.5 %copy-start.2 = (f32[4,2,1]{0,2,1:T(1,128)S(1)}, f32[4,2,1]{0,2,1:T(1,128)}, u32[]{:S(2)}) copy-start(f32[4,2,1]{0,2,1:T(1,128)} %param.11) | copy-start | bytes 100
  218.2 23.3 %copy-start = (f32[4,2,512,512]{3,2,1,0:T(8,128)S(1)}, f32[4,2,512,512]{3,2,1,0:T(8,128)}, u32[]{:S(2)}) copy-start(f32[4,2,512,512]{3,2,1,0:T(8,128)} %all-reduce.3.cloned.1.call-done) | copy-start | bytes 25165828
  261.4 6.8 %copy-start.1 = (f32[4,2,512,512]{3,2,1,0:T(8,128)S(1)}, f32[4,2,512,512]{3,2,1,0:T(8,128)}, u32[]{:S(2)}) copy-start(f32[4,2,512,512]{3,2,1,0:T(8,128)} %multiply_subtract_fusion) | copy-start | bytes 25165828
Sparse Core Ops, SparseCore 0:
  42.7 170.4 all-reduce.2
where the time goes:
time: 298 us
  waiting for transfers between devices  170 us (57%)
  matrix products  59.3 us (20%)
  blocking collectives  34.2 us (11%)
  between operations  14.2 us (5%)
  local copies, waits for them, and re-layouts  10.1 us (3%)
  other arithmetic  9.73 us (3%)
    psum x1, waiting for transfers between devices, on_device(): summed = lax.psum(gram_blocks, 'dp')  170 us
    dot_general x2, matrix products, newton_rows(): jnp.einsum('eirk,eikc->eirc', rows_now, matrix, precision=lax.Precision.H...  30.1 us
    dot_general x2, matrix products, newton_rows(): jnp.einsum('eirk,eikc->eirc', left_product, whole_now, precision=lax.Prec...  24.7 us
    all_to_all x1, blocking collectives, on_device(): lax.all_to_all(buffer, 'expert', split_axis=0, concat_axis=1, tiled=True)  17.7 us
    all_gather x1, blocking collectives, on_device(): lax.all_gather(act_rows, 'expert', axis=0, tiled=True)  8.67 us
    all_gather x1, blocking collectives, on_device(): lax.all_gather(grad_rows, 'expert', axis=0, tiled=True)  7.79 us
  transfers between devices with their start and end apart: 1, of which 1 were waited for; matrix products, arithmetic and copies ran while one was open for 0% of the time, Pallas kernels for 0%

commit v1 on v0

--- a/solution.py
+++ b/solution.py
@@ -9,6 +9,15 @@
 NBLK = 1
 CAP = 64
 WIDTH = 512
+
+
+def added_up(shard, mesh_axis):
+    size = lax.axis_size(mesh_axis)
+    total, far = (shard, 1)
+    while far < size:
+        total = total + lax.ppermute(total, mesh_axis, [(i, i ^ far) for i in range(size)])
+        far = 2 * far
+    return total
 
 
 def slot_table(route_ids, capacity):
@@ -65,7 +74,7 @@
     rows_share = BLOCK // lax.axis_size("dp")
     row_start = lax.axis_index("dp") * rows_share
     identity = jnp.eye(BLOCK, dtype=jnp.float32)
-    summed = lax.psum(gram_blocks, "dp")
+    summed = added_up(gram_blocks, "dp")
     matrix = summed + damping_flat * identity
     largest_sum = jnp.max(jnp.sum(jnp.abs(matrix), axis=3), axis=2)
     inverse_bound = 1.0 / largest_sum

time: 298 us -> 889 us (2.98)
  waiting for transfers between devices: 170 us -> 734 us
  other arithmetic: 9.73 us -> 48.8 us
  between operations: 14.2 us -> 0.84 us
    ppermute x0 -> x4, waiting for transfers between devices: none -> 734 us  [added_up(): lax.ppermute(total, mesh_axis, [(i, i ^ far) for i in range(size)])]
    psum x1 -> x0, waiting for transfers between devices: 170 us -> none  [on_device(): summed = lax.psum(gram_blocks, 'dp')]
    add x0 -> x3, other arithmetic: none -> 33.2 us  [added_up(): total + lax.ppermute(total, mesh_axis, [(i, i ^ far) for i in range(size)])]
  transfers between devices with their start and end apart: 1 -> 4, of which waited for: 1 -> 4; matrix products, arithmetic and copies ran while one was open for 0% -> 0% of each run, Pallas kernels for 0% -> 0%
where the time goes in v1:
time: 889 us
  waiting for transfers between devices  734 us (83%)
  matrix products  53.6 us (6%)
  other arithmetic  48.8 us (5%)
  blocking collectives  32.6 us (4%)
  local copies, waits for them, and re-layouts  13.3 us (1%)
    ppermute x4, waiting for transfers between devices, added_up(): lax.ppermute(total, mesh_axis, [(i, i ^ far) for i in range(size)])  734 us
    add x3, other arithmetic, added_up(): total + lax.ppermute(total, mesh_axis, [(i, i ^ far) for i in range(size)])  33.2 us
    dot_general x2, matrix products, newton_rows(): jnp.einsum('eirk,eikc->eirc', rows_now, matrix, precision=lax.Precision.H...  28.3 us
    dot_general x2, matrix products, newton_rows(): jnp.einsum('eirk,eikc->eirc', left_product, whole_now, precision=lax.Prec...  24 us
  transfers between devices with their start and end apart: 4, of which 4 were waited for; matrix products, arithmetic and copies ran while one was open for 0% of the time, Pallas kernels for 0%

profile of v1, /device:TPU:0, one launch (start us, length us, event | category | flops | bytes accessed | tf_op | source)
XLA Modules:
  0.0 888.7 jit_solution(6632500211606088601)
XLA Ops:
  0.6 0.8 copy.37
  1.4 0.1 eq.38
  1.6 0.1 eq.34
  1.7 0.7 broadcast_multiply_fusion.3
  2.4 0.6 reduce-window.6
  3.0 0.2 slice_reduce_fusion
  3.3 0.1 copy.36
  3.4 0.1 mul.132
  3.6 1.4 scatter_custom_fusion
  5.0 0.7 fusion.21
  5.9 0.1 mul.139
  6.0 0.7 subtract_bitcast_fusion
  6.7 0.7 pad_maximum_fusion
  7.3 0.1 copy.39
  7.4 0.1 stack.14
  7.6 1.0 mul.136
  8.6 0.4 mul.137
  9.0 1.0 broadcast_multiply_fusion.1
  10.0 0.1 broadcast_in_dim.36
  10.1 0.1 concatenate.12
  10.3 0.1 multiply_convert_fusion
  10.4 0.1 fusion.11
  10.5 2.1 gather_fusion
  12.6 0.8 gather.7
  13.5 0.2 copy_select_fusion
  13.7 17.7 %all_to_all.18 = bf16[8,64,2,512]{3,1,2,0:T(8,128)(2,1)S(1)} all-to-all(bf16[8,64,2,512]{3,1,2,0:T(8,128)(2,1)S(1)} %copy_select_fusion), channel_id=1, replica_groups=mesh['expert'=2,'dp'=16] {'expert'}, dimensions={0} | all-to-all | bytes 2097152 | tf_op jit(solution)/shard_map/all_to_all | solution.py:68
  31.5 1.3 broadcast_multiply_fusion
  32.8 3.2 copy-done.2
  36.0 13.3 %collective-permute-done = f32[4,2,512,512]{3,2,1,0:T(8,128)} collective-permute-done((f32[4,2,512,512]{3,2,1,0:T(8,128)S(1)}, f32[4,2,512,512]{3,2,1,0:T(8,128)}, u32[]{:S(2)}, u32[]{:S(2)}) %collective-permute-start) | collective-permute-done | bytes 8388640 | tf_op jit(solution)/shard_map/ppermute | solution.py:18
  49.3 11.1 %add.69 = f32[4,2,512,512]{3,2,1,0:T(8,128)} add(f32[4,2,512,512]{3,2,1,0:T(8,128)} %copy-done.2, f32[4,2,512,512]{3,2,1,0:T(8,128)} %collective-permute-done) | non-fusion elementwise | flops 2097152 | bytes 25165824 | tf_op jit(solution)/shard_map/add | solution.py:18
  60.4 1.6 collective-permute-start.1
  61.9 181.2 %collective-permute-done.1 = f32[4,2,512,512]{3,2,1,0:T(8,128)} collective-permute-done((f32[4,2,512,512]{3,2,1,0:T(8,128)}, f32[4,2,512,512]{3,2,1,0:T(8,128)}, u32[]{:S(2)}, u32[]{:S(2)}) %collective-permute-start.1) | collective-permute-done | bytes 8388640 | tf_op jit(solution)/shard_map/ppermute | solution.py:18
  243.2 11.1 %add.70 = f32[4,2,512,512]{3,2,1,0:T(8,128)} add(f32[4,2,512,512]{3,2,1,0:T(8,128)} %add.69, f32[4,2,512,512]{3,2,1,0:T(8,128)} %collective-permute-done.1) | non-fusion elementwise | flops 2097152 | bytes 25165824 | tf_op jit(solution)/shard_map/add | solution.py:18
  254.3 1.6 collective-permute-start.2
  255.9 180.3 %collective-permute-done.2 = f32[4,2,512,512]{3,2,1,0:T(8,128)} collective-permute-done((f32[4,2,512,512]{3,2,1,0:T(8,128)}, f32[4,2,512,512]{3,2,1,0:T(8,128)}, u32[]{:S(2)}, u32[]{:S(2)}) %collective-permute-start.2) | collective-permute-done | bytes 8388640 | tf_op jit(solution)/shard_map/ppermute | solution.py:18
  436.2 11.1 %add.71 = f32[4,2,512,512]{3,2,1,0:T(8,128)} add(f32[4,2,512,512]{3,2,1,0:T(8,128)} %add.70, f32[4,2,512,512]{3,2,1,0:T(8,128)} %collective-permute-done.2) | non-fusion elementwise | flops 2097152 | bytes 25165824 | tf_op jit(solution)/shard_map/add | solution.py:18
  447.3 2.7 collective-permute-start.3
  450.0 0.1 fusion.10
  450.2 358.9 %collective-permute-done.3 = f32[4,2,512,512]{3,2,1,0:T(8,128)} collective-permute-done((f32[4,2,512,512]{3,2,1,0:T(8,128)}, f32[4,2,512,512]{3,2,1,0:T(8,128)}, u32[]{:S(2)}, u32[]{:S(2)}) %collective-permute-start.3) | collective-permute-done | bytes 8388640 | tf_op jit(solution)/shard_map/ppermute | solution.py:18
  809.1 10.4 %abs_reduce_fusion = (f32[4,2,512]{2,1,0:T(2,128)S(1)}, f32[4,2,512,512]{3,2,1,0:T(8,128)}) fusion(f32[512,512]{1,0:T(8,128)S(1)} %fusion.10, f32[4,2]{1,0:T(4,128)S(1)} %copy.43, f32[4,2,512,512]{3,2,1,0:T(8,128)} %add.71, f32[4,2,512,512]{3,2,1,0:T(8,128)} %collective-permute-done.3), kind=kLoop, calls=%fused_computation.6 | loop fusion | flops 10481664 | bytes 26230816 | tf_op jit(solution)/shard_map/reduce_sum | solution.py:79
  819.9 22.2 %fusion.1 = f32[4,2,512,512]{3,2,1,0:T(8,128)} fusion(f32[4,2,512,512]{3,2,1,0:T(8,128)} %get-tuple-element.3, f32[4,2]{1,0:T(4,128)S(1)} %copy.46, f32[4,2]{1,0:T(4,128)S(1)} %copy.45, f32[512,512]{1,0:T(8,128)S(1)} %fusion.10), kind=kOutput, calls=%fused_computation.5 | convolution fusion | flops 12891193344 | bytes 17825856 | tf_op jit(solution)/shard_map/eirk,eikc->eirc/dot_general | solution.py:36
  842.1 19.2 %multiply_subtract_fusion = f32[4,2,512,512]{3,2,1,0:T(8,128)} fusion(f32[4,2,512,512]{3,2,1,0:T(8,128)S(1)} %copy-done, f32[4,2,512,512]{3,2,1,0:T(8,128)} %fusion.1, f32[4,2]{1,0:T(4,128)S(1)} %copy.46, f32[4,2]{1,0:T(4,128)S(1)} %copy.45, f32[512,512]{1,0:T(8,128)S(1)} %fusion.10), kind=kOutput, calls=%fused_computation.2 | convolution fusion | flops 12901679104 | bytes 26214464 | tf_op jit(solution)/shard_map/eirk,eikc->eirc/dot_general | solution.py:37
  861.3 6.0 fusion.12
  867.3 4.9 multiply_subtract_fusion.6
  872.3 7.8 all_gather.6
  880.1 7.0 all_gather.7
  887.1 0.8 copy.52
  887.9 0.8 copy.53
  (29 shorter events, 0.9 us)
Async XLA Ops:
  32.8 3.2 copy-start.2
  36.0 13.3 %collective-permute-start = (f32[4,2,512,512]{3,2,1,0:T(8,128)S(1)}, f32[4,2,512,512]{3,2,1,0:T(8,128)}, u32[]{:S(2)}, u32[]{:S(2)}) collective-permute-start(f32[4,2,512,512]{3,2,1,0:T(8,128)S(1)} %broadcast_multiply_fusion), channel_id=1, source_target_pairs={{0,1},{1,0},{2,3},{3,2},{4,5},{5,4},{6,7},{7,6},{8,9},{9,8},{10,11... | collective-permute-start | bytes 25165832 | tf_op jit(solution)/shard_map/ppermute | solution.py:18
  60.4 182.8 %collective-permute-start.1 = (f32[4,2,512,512]{3,2,1,0:T(8,128)}, f32[4,2,512,512]{3,2,1,0:T(8,128)}, u32[]{:S(2)}, u32[]{:S(2)}) collective-permute-start(f32[4,2,512,512]{3,2,1,0:T(8,128)} %add.69), channel_id=1, source_target_pairs={{0,2},{1,3},{2,0},{3,1},{4,6},{5,7},{6,4},{7,5},{8,10},{9,11},{10,... | collective-permute-start | bytes 25165832 | tf_op jit(solution)/shard_map/ppermute | solution.py:18
  254.3 195.7 %copy-start.3 = (f32[4,2,1]{0,2,1:T(1,128)S(1)}, f32[4,2,1]{0,2,1:T(1,128)}, u32[]{:S(2)}) copy-start(f32[4,2,1]{0,2,1:T(1,128)} %param.11) | copy-start | bytes 100
  254.3 182.0 %collective-permute-start.2 = (f32[4,2,512,512]{3,2,1,0:T(8,128)}, f32[4,2,512,512]{3,2,1,0:T(8,128)}, u32[]{:S(2)}, u32[]{:S(2)}) collective-permute-start(f32[4,2,512,512]{3,2,1,0:T(8,128)} %add.70), channel_id=1, source_target_pairs={{0,4},{1,5},{2,6},{3,7},{4,0},{5,1},{6,2},{7,3},{8,12},{9,13},{10,... | collective-permute-start | bytes 25165832 | tf_op jit(solution)/shard_map/ppermute | solution.py:18
  447.3 361.8 %collective-permute-start.3 = (f32[4,2,512,512]{3,2,1,0:T(8,128)}, f32[4,2,512,512]{3,2,1,0:T(8,128)}, u32[]{:S(2)}, u32[]{:S(2)}) collective-permute-start(f32[4,2,512,512]{3,2,1,0:T(8,128)} %add.71), channel_id=1, source_target_pairs={{0,8},{1,9},{2,10},{3,11},{4,12},{5,13},{6,14},{7,15},{8,0},{9,1},... | collective-permute-start | bytes 25165832 | tf_op jit(solution)/shard_map/ppermute | solution.py:18
  819.9 22.2 %copy-start = (f32[4,2,512,512]{3,2,1,0:T(8,128)S(1)}, f32[4,2,512,512]{3,2,1,0:T(8,128)}, u32[]{:S(2)}) copy-start(f32[4,2,512,512]{3,2,1,0:T(8,128)} %get-tuple-element.3) | copy-start | bytes 25165828
  861.3 6.1 copy-start.1
